TPU v7x, 128 devices: a whole 4x4x4 slice. The times are simulated.
128 devices in a mesh: pts: 64 (over z, y, x), rows: 2 (over core).
Axes of the slice: x: 4, y: 4, z: 4, core: 2. Of those that a mesh axis runs over, the one named last changes fastest.
Arguments:
- vertex: bfloat16 [64, 960, 960], P('pts', 'rows'), may hold values from -0.1875 to 0.1875
- bubble: float32 [64, 960], P('pts'), may hold values from -2 to -0.2
- cross_deriv: bfloat16 [64, 960, 960], P('pts', 'rows'), may hold values from -6 to 6
- send_blocks: int32 [64, 64, 2], P('pts'), may hold values from -1 to 14, as said below
- recv_slots: int32 [64, 15], P('pts'), may hold values from 0 to 127, as said below
- freq_shift: int32 [64, 15], P('pts'), may hold values from -16 to 16
- proj_coef: float32 [64, 15], P('pts'), may hold values from -1.5 to 1.5
Outputs:
- left_insertion: bfloat16 [64, 960, 960], P('pts', 'rows')
Inputs may be any that keep to these rules, and one draw needn't show every extreme that they name: `send_blocks`: entry [d, e, c] is -1 for an empty slot, else the index p * 15 + g of the box (local point p, form factor g) of device d along pts that fills slot c towards device e. For every e some d fills all 2 slots towards e. `recv_slots`: entry [q, f] is 2 * d + c for a slot c towards device q // 1 along pts whose send_blocks entry [d, q, c] is not -1; each such slot is named by exactly one entry of that device's points.
All inputs are finite; a program needn't handle non-finite values.
Results may differ from a plain program's by a relative error of at most 0.0058.
Values may be sent and summed in bfloat16 or wider, within the bound.
A program may use at most 128 MiB of HBM per device.

v0:
```python
import jax
import jax.numpy as jnp
from jax import lax
from jax.sharding import PartitionSpec as P


def copy_for_each(array, axis):
    copies = jnp.broadcast_to(array, (lax.axis_size(axis), *array.shape))
    return lax.all_to_all(copies, axis, split_axis=0, concat_axis=0, tiled=True)


def in_order(parts, dim):
    parts = jnp.moveaxis(parts, 0, dim)
    dims = parts.shape
    return parts.reshape(*dims[:dim], dims[dim] * dims[dim + 1], *dims[dim + 2 :])


def collect(array, axis, dim):
    parts = copy_for_each(array, axis)
    return in_order(parts, dim)


def add_rows(left_cols, panel):
    return jnp.dot(left_cols, panel, preferred_element_type=jnp.float32)


def body(vertex, bubble, cross_deriv, send_blocks, recv_slots, freq_shift, proj_coef):
    points, rows_here, width_all = vertex.shape
    form_count = recv_slots.shape[1]
    matsubara_number = width_all // form_count
    local_boxes = cross_deriv.reshape(points, rows_here, form_count, matsubara_number).transpose(
        0, 2, 1, 3
    )
    local_boxes = local_boxes.reshape(points * form_count, rows_here, matsubara_number)
    wanted = send_blocks[0]
    outgoing = jnp.where(
        (wanted >= 0)[:, :, None, None],
        local_boxes[jnp.clip(wanted, 0, points * form_count - 1)],
        jnp.zeros((), jnp.bfloat16),
    )
    incoming = lax.all_to_all(outgoing, "pts", split_axis=0, concat_axis=0, tiled=True)
    arrived = incoming.reshape(-1, rows_here, matsubara_number)
    picked = arrived[recv_slots]
    source_grid = jnp.arange(matsubara_number, dtype=jnp.int32)
    target_freq = source_grid[None, None, None, :] + freq_shift[:, :, None, None]
    selector = (source_grid[None, None, :, None] == target_freq).astype(jnp.bfloat16)
    shifted = jnp.einsum("pfrm,pfmn->pfrn", picked, selector, preferred_element_type=jnp.float32)
    box_values = (shifted * proj_coef[:, :, None, None]).astype(jnp.bfloat16)
    remapped = box_values.transpose(0, 2, 1, 3).reshape(points, rows_here, width_all)
    scaled = (vertex.astype(jnp.float32) * bubble[:, None, :]).astype(jnp.bfloat16)
    outputs = [add_rows(scaled[0], collect(remapped[0], "rows", 0))]
    result = jnp.stack(outputs)
    return result.astype(jnp.bfloat16)


def solution(mesh):
    in_specs = (
        P("pts", "rows", None),
        P("pts", None),
        P("pts", "rows", None),
        P("pts", None, None),
        P("pts", None),
        P("pts", None),
        P("pts", None),
    )
    out_specs = P("pts", "rows", None)
    return jax.shard_map(body, mesh=mesh, in_specs=in_specs, out_specs=out_specs, check_vma=False)
```

profile of v0, /device:TPU:1, one launch (start us, length us, event | category | flops | bytes accessed | tf_op | source)
XLA Modules:
  0.0 159.4 jit_solution(16579774778318162401)
XLA Ops:
  0.0 0.7 compare_select_fusion
  0.7 0.7 compare_bitcast_fusion
  1.4 1.7 %copy.12 = bf16[1,480,960]{1,2,0:T(8,128)(2,1)S(1)} copy(bf16[1,480,960]{2,1,0:T(8,128)(2,1)} %param.9) | data formatting | bytes 1843200 | tf_op args[2]
  3.0 0.1 copy.13
  3.1 0.1 reshape.90
  3.3 0.1 copy.11
  3.4 6.2 %gather_fusion = bf16[128,480,64]{1,2,0:T(8,128)(2,1)} fusion(bf16[15,480,64]{1,2,0:T(8,128)(2,1)S(1)} %bitcast.31, s32[1024]{0:T(1024)S(1)} %pad_clamp_fusion.1), kind=kCustom, calls=%fused_computation | custom fusion | bytes 15729152 | tf_op jit(solution)/shard_map/gather | solution.py:38
  9.6 7.2 %broadcast_select_fusion = bf16[64,2,480,64]{2,3,1,0:T(8,128)(2,1)} fusion(bf16[64,2,480,64]{2,3,1,0:T(8,128)(2,1)} %bitcast.32, pred[64,2]{1,0:T(8,128)(4,1)S(1)} %copy.11), kind=kLoop, calls=%fused_computation.2 | loop fusion | flops 3932160 | bytes 15728768 | tf_op jit(solution)/shard_map/jit(_where)/select_n | solution.py:36
  16.9 0.0 copy-start.4
  16.9 0.0 copy-start.1
  16.9 12.4 %all-to-all-start = ((bf16[64,2,480,64]{2,3,1,0:T(8,128)(2,1)}), bf16[64,2,480,64]{2,3,1,0:T(8,128)(2,1)}, u32[]{:S(2)}, u32[]{:S(2)}) async-start(bf16[64,2,480,64]{2,3,1,0:T(8,128)(2,1)} %broadcast_select_fusion), calls=%async_computation | async-start | bytes 16777216 | tf_op jit(solution)/shard_map/all_to_all | solution.py:41
  29.3 0.0 copy-done.4
  29.3 0.0 copy-start
  29.3 0.0 copy-done.1
  29.3 0.1 iota_add_fusion
  29.4 115.9 %all-to-all-done = bf16[64,2,480,64]{2,3,1,0:T(8,128)(2,1)} async-done(((bf16[64,2,480,64]{2,3,1,0:T(8,128)(2,1)}), bf16[64,2,480,64]{2,3,1,0:T(8,128)(2,1)}, u32[]{:S(2)}, u32[]{:S(2)}) %all-to-all-start) | async-done | bytes 7864352 | tf_op jit(solution)/shard_map/all_to_all | solution.py:41
  145.3 4.0 %gather_fusion.1 = bf16[15,480,64]{1,2,0:T(8,128)(2,1)S(1)} fusion(bf16[128,480,64]{1,2,0:T(8,128)(2,1)} %bitcast.8, s32[1024]{0:T(1024)S(1)} %pad_clamp_fusion), kind=kCustom, calls=%fused_computation.1 | custom fusion | bytes 1843260 | tf_op jit(solution)/shard_map/gather | solution.py:43
  149.3 0.0 copy-done
  149.3 0.5 multiply_convert_fusion
  149.8 0.7 copy.14
  150.4 0.2 broadcast_in_dim.28
  150.7 0.0 copy-start.2
  150.7 0.0 copy-start.3
  150.7 6.6 %all_to_all.10 = bf16[2,480,960]{2,1,0:T(8,128)(2,1)S(1)} all-to-all(bf16[2,480,960]{2,1,0:T(8,128)(2,1)S(1)} %broadcast_in_dim.28), channel_id=1, replica_groups=mesh['pts'=64,'rows'=2] {'rows'}, dimensions={0} | all-to-all | bytes 3686400 | tf_op jit(solution)/shard_map/all_to_all | solution.py:9
  157.3 0.0 copy-done.2
  157.3 0.0 copy-done.3
  157.3 2.1 %fusion = bf16[1,480,960]{2,1,0:T(8,128)(2,1)} fusion(bf16[960,960]{1,0:T(8,128)(2,1)S(1)} %bitcast.34, bf16[1,480,960]{2,1,0:T(8,128)(2,1)S(1)} %copy-done.2, f32[960]{0:T(1024)S(1)} %bitcast.37), kind=kOutput, calls=%fused_computation.6 | convolution fusion | flops 886579200 | bytes 3690240 | tf_op jit(solution)/shard_map/dot_general | solution.py:24
  (3 shorter events, 0.0 us)
Async XLA Ops:
  16.9 12.4 %copy-start.4 = (s32[1,15]{1,0:T(1,128)S(1)}, s32[1,15]{1,0:T(1,128)}, u32[]{:S(2)}) copy-start(s32[1,15]{1,0:T(1,128)} %param.11) | copy-start | bytes 184
  16.9 12.4 %copy-start.1 = (s32[1,15]{1,0:T(1,128)S(1)}, s32[1,15]{1,0:T(1,128)}, u32[]{:S(2)}) copy-start(s32[1,15]{1,0:T(1,128)} %param.12) | copy-start | bytes 184
  16.9 128.4 %all-to-all-start = ((bf16[64,2,480,64]{2,3,1,0:T(8,128)(2,1)}), bf16[64,2,480,64]{2,3,1,0:T(8,128)(2,1)}, u32[]{:S(2)}, u32[]{:S(2)}) async-start(bf16[64,2,480,64]{2,3,1,0:T(8,128)(2,1)} %broadcast_select_fusion), calls=%async_computation | async-start | bytes 16777216 | tf_op jit(solution)/shard_map/all_to_all | solution.py:41
  29.3 120.0 %copy-start = (f32[1,15]{1,0:T(1,128)S(1)}, f32[1,15]{1,0:T(1,128)}, u32[]{:S(2)}) copy-start(f32[1,15]{1,0:T(1,128)} %param.13) | copy-start | bytes 184
  150.7 6.6 %copy-start.2 = (bf16[1,480,960]{2,1,0:T(8,128)(2,1)S(1)}, bf16[1,480,960]{2,1,0:T(8,128)(2,1)}, u32[]{:S(2)}) copy-start(bf16[1,480,960]{2,1,0:T(8,128)(2,1)} %param.7) | copy-start | bytes 2764804
  150.7 6.6 %copy-start.3 = (f32[1,960]{1,0:T(1,128)S(1)}, f32[1,960]{1,0:T(1,128)}, u32[]{:S(2)}) copy-start(f32[1,960]{1,0:T(1,128)} %param.8) | copy-start | bytes 11524
where the time goes:
time: 162 us; the launch traced here: 159 us
  waiting for transfers between devices  116 us (72%)
  local copies, waits for them, and re-layouts  13.2 us (8%)
  starting transfers between devices  12.4 us (8%)
  other arithmetic  8.69 us (5%)
  blocking collectives  6.56 us (4%)
  matrix products  2.61 us (2%)
    all_to_all x1, waiting for transfers between devices, body(): lax.all_to_all(outgoing, 'pts', split_axis=0, concat_axis=0, tiled=True)  116 us
    all_to_all x1, starting transfers between devices, body(): lax.all_to_all(outgoing, 'pts', split_axis=0, concat_axis=0, tiled=True)  12.4 us
    select_n x1, other arithmetic, body(): jnp.where((wanted >= 0)[:, :, None, None], local_boxes[jnp.clip(wanted, 0...  7.24 us
    all_to_all x1, blocking collectives, copy_for_each(): return lax.all_to_all(copies, axis, split_axis=0, concat_axis=0, tiled=True)  6.56 us
    gather x1, local copies, waits for them, and re-layouts, body(): local_boxes[jnp.clip(wanted, 0, points * form_count - 1)]  6.23 us
    gather x1, local copies, waits for them, and re-layouts, body(): picked = arrived[recv_slots]  3.99 us
  transfers between devices with their start and end apart: 1, of which 1 were waited for; matrix products, arithmetic and copies ran while one was open for 0% of the time, Pallas kernels for 0%

commit v1 on v0

v1 whole, which is shorter than its diff:
```python
import jax
import jax.numpy as jnp
from jax import lax
from jax.sharding import PartitionSpec as P

SLOTS = 16


def exchange(array, axis):
    return lax.all_to_all(array, axis, split_axis=0, concat_axis=0, tiled=True)


def body(vertex, bubble, cross_deriv, send_blocks, recv_slots, freq_shift, proj_coef):
    _, rows, width = vertex.shape
    forms = recv_slots.shape[1]
    freqs = width // forms
    points = send_blocks.shape[1]
    cap = send_blocks.shape[2]
    f32, bf16 = jnp.float32, jnp.bfloat16

    boxes = cross_deriv[0].reshape(rows, forms, freqs).transpose(2, 1, 0)
    table = jnp.concatenate([send_blocks[0].T.reshape(-1), recv_slots[0]]).astype(bf16)
    table = jnp.pad(table, (0, rows - table.shape[0]))
    table = jnp.broadcast_to(table[None, None], (freqs, 1, rows))
    got = exchange(jnp.concatenate([boxes, table], axis=1), "pts")

    tables = got[:, forms, :]
    sb = tables[:, : cap * points].astype(f32).reshape(points, cap, points)
    rs = tables[:, cap * points : cap * points + forms].astype(f32)
    rs = jnp.pad(rs, ((0, 0), (0, SLOTS - forms)), constant_values=-1.0)
    source = jnp.arange(points * SLOTS, dtype=jnp.int32)
    src_dev = (source // SLOTS).astype(f32)
    src_form = (source % SLOTS).astype(f32)
    pick = jnp.zeros((points, SLOTS, points * SLOTS), jnp.bool_)
    for c in range(cap):
        held = jnp.repeat(sb[:, c, :].T, SLOTS, axis=1)
        slot = jnp.where(held == src_form[None], src_dev[None] * cap + c, -2.0)
        pick = pick | (rs[:, :, None] == slot[:, None, :])
    pick = pick.astype(bf16).reshape(points * SLOTS, points * SLOTS)
    chosen = jnp.dot(pick, got.reshape(points * SLOTS, rows), preferred_element_type=f32)
    chosen = chosen.astype(bf16).reshape(points, SLOTS, rows)
    mine = exchange(chosen, "pts").reshape(freqs * SLOTS, rows)

    line = jnp.arange(freqs * SLOTS, dtype=jnp.int32)
    column = jnp.arange(width, dtype=jnp.int32)
    wanted_n = column % freqs + jnp.repeat(freq_shift[0], freqs)
    wanted = jnp.where(
        (wanted_n >= 0) & (wanted_n < freqs), wanted_n * SLOTS + column // freqs, -1
    )
    shift = (line[:, None] == wanted[None, :]).astype(bf16)
    moved = lax.dot_general(mine, shift, (((0,), (0,)), ((), ())), preferred_element_type=f32)
    remapped = (moved * jnp.repeat(proj_coef[0], freqs)[None]).astype(bf16)
    both = exchange(jnp.broadcast_to(remapped, (2, rows, width)), "rows").reshape(2 * rows, width)
    scaled = (vertex[0].astype(f32) * bubble[0][None]).astype(bf16)
    out = jnp.dot(scaled, both, preferred_element_type=f32)
    return out.astype(bf16)[None]


def solution(mesh):
    in_specs = (
        P("pts", "rows", None),
        P("pts", None),
        P("pts", "rows", None),
        P("pts", None, None),
        P("pts", None),
        P("pts", None),
        P("pts", None),
    )
    out_specs = P("pts", "rows", None)
    return jax.shard_map(body, mesh=mesh, in_specs=in_specs, out_specs=out_specs, check_vma=False)
```

time: 162 us -> 72.7 us (0.45); the launches traced: 159 us -> 72.4 us
  waiting for transfers between devices: 116 us -> 34 us
  local copies, waits for them, and re-layouts: 13.2 us -> 5.86 us
  other arithmetic: 8.69 us -> 2.75 us
  starting transfers between devices: 12.4 us -> 16.6 us
  matrix products: 2.61 us -> 4.61 us
  blocking collectives: 6.56 us -> 8.3 us
    all_to_all x1 -> x2, waiting for transfers between devices: 116 us -> 34 us  [exchange(): return lax.all_to_all(array, axis, split_axis=0, concat_axis=0, tiled=True)]
    gather x2 -> x0, local copies, waits for them, and re-layouts: 10.2 us -> none  [the longest x1 6.23 us: body(): local_boxes[jnp.clip(wanted, 0, points * form_count - 1)]]
    select_n x2, other arithmetic: 7.92 us -> 0.48 us  [the longest x1 0.47 us: body(): slot = jnp.where(held == src_form[None], src_dev[None] * cap + c, -2.0)]
    all_to_all x1 -> x2, starting transfers between devices: 12.4 us -> 16.6 us  [exchange(): return lax.all_to_all(array, axis, split_axis=0, concat_axis=0, tiled=True)]
    dot_general x2 -> x3, matrix products: 2.61 us -> 4.61 us  [the longest x1 2.14 us: body(): out = jnp.dot(scaled, both, preferred_element_type=f32)]
    all_to_all x1, blocking collectives: 6.56 us -> 8.3 us  [exchange(): return lax.all_to_all(array, axis, split_axis=0, concat_axis=0, tiled=True)]
  transfers between devices with their start and end apart: 1 -> 2, of which waited for: 1 -> 2; matrix products, arithmetic and copies ran while one was open for 0% -> 0% of each run, Pallas kernels for 0% -> 0%
where the time goes in v1:
time: 72.7 us; the launch traced here: 72.4 us
  waiting for transfers between devices  34 us (47%)
  starting transfers between devices  16.6 us (23%)
  blocking collectives  8.3 us (11%)
  local copies, waits for them, and re-layouts  5.86 us (8%)
  matrix products  4.61 us (6%)
  other arithmetic  2.75 us (4%)
    all_to_all x2, waiting for transfers between devices, exchange(): return lax.all_to_all(array, axis, split_axis=0, concat_axis=0, tiled=True)  34 us
    all_to_all x2, starting transfers between devices, exchange(): return lax.all_to_all(array, axis, split_axis=0, concat_axis=0, tiled=True)  16.6 us
    all_to_all x1, blocking collectives, exchange(): return lax.all_to_all(array, axis, split_axis=0, concat_axis=0, tiled=True)  8.3 us
    dot_general x1, matrix products, body(): out = jnp.dot(scaled, both, preferred_element_type=f32)  2.14 us
    unnamed x10, local copies, waits for them, and re-layouts  1.71 us
    concatenate x1, local copies, waits for them, and re-layouts, body(): got = exchange(jnp.concatenate([boxes, table], axis=1), 'pts')  1.55 us
  transfers between devices with their start and end apart: 2, of which 2 were waited for; matrix products, arithmetic and copies ran while one was open for 0% of the time, Pallas kernels for 0%

profile of v1, /device:TPU:1, one launch (start us, length us, event | category | flops | bytes accessed | tf_op | source)
XLA Modules:
  0.0 72.4 jit_solution(14427502243139192584)
XLA Ops:
  0.0 0.7 convert_bitcast_fusion.1
  0.7 0.1 reshape.222
  0.8 0.7 convert_bitcast_fusion
  1.4 1.7 %copy.14 = bf16[1,480,960]{1,2,0:T(8,128)(2,1)S(1)} copy(bf16[1,480,960]{2,1,0:T(8,128)(2,1)} %param.9) | data formatting | bytes 1843200 | tf_op args[2]
  3.1 0.1 pad_maximum_fusion
  3.3 1.6 %copy.15 = bf16[64,16,480]{2,1,0:T(8,128)(2,1)} copy(bf16[64,16,480]{2,0,1:T(8,128)(2,1)S(1)} %pad_maximum_fusion) | data formatting | bytes 1966080 | tf_op jit(solution)/shard_map/concatenate | solution.py:25
  4.8 12.0 %all-to-all-start = ((bf16[64,16,480]{2,1,0:T(8,128)(2,1)}), bf16[64,16,480]{2,1,0:T(8,128)(2,1)S(1)}, u32[]{:S(2)}, u32[]{:S(2)}) async-start(bf16[64,16,480]{2,1,0:T(8,128)(2,1)} %copy.15), calls=%async_computation | async-start | bytes 2097152 | tf_op jit(solution)/shard_map/all_to_all | solution.py:10
  16.8 17.7 %all-to-all-done = bf16[64,16,480]{2,1,0:T(8,128)(2,1)S(1)} async-done(((bf16[64,16,480]{2,1,0:T(8,128)(2,1)}), bf16[64,16,480]{2,1,0:T(8,128)(2,1)S(1)}, u32[]{:S(2)}, u32[]{:S(2)}) %all-to-all-start) | async-done | bytes 983072 | tf_op jit(solution)/shard_map/all_to_all | solution.py:10
  34.5 0.1 slice.20
  34.7 0.1 reshape.233
  34.8 0.1 fusion.27
  34.9 0.5 fusion.6
  35.3 0.2 copy.17
  35.5 0.2 copy.18
  35.7 0.8 %compare_or_fusion = pred[64,16,1024]{2,1,0:T(8,128)(4,1)S(1)} fusion(f32[64,1024]{1,0:T(8,128)S(1)} %copy.18, f32[64,1024]{1,0:T(8,128)S(1)} %copy.17, f32[64,16]{1,0:T(8,128)S(1)} %pad_convert_fusion), kind=kLoop, calls=%fused_computation.2 | loop fusion | flops 3145728 | bytes 1576960 | tf_op jit(solution)/shard_map/or | solution.py:38
  36.5 1.2 %convolution_convert_fusion.1 = bf16[1024,480]{0,1:T(8,128)(2,1)S(1)} fusion(pred[1024,1024]{1,0:T(8,128)(4,1)S(1)} %bitcast.47, bf16[1024,480]{1,0:T(8,128)(2,1)S(1)} %bitcast.45), kind=kOutput, calls=%fused_computation.7 | convolution fusion | flops 1007124480 | bytes 3014656 | tf_op jit(solution)/shard_map/dot_general | solution.py:40
  37.8 0.0 copy-start
  37.8 0.0 copy-start.1
  37.8 1.3 %copy.19 = bf16[1024,480]{1,0:T(8,128)(2,1)} copy(bf16[1024,480]{0,1:T(8,128)(2,1)S(1)} %convolution_convert_fusion.1) | data formatting | bytes 1966080 | tf_op jit(solution)/shard_map/convert_element_type | solution.py:41
  39.1 4.7 %all-to-all-start.1 = ((bf16[64,16,480]{2,1,0:T(8,128)(2,1)}), bf16[64,16,480]{2,1,0:T(8,128)(2,1)S(1)}, u32[]{:S(2)}, u32[]{:S(2)}) async-start(bf16[64,16,480]{2,1,0:T(8,128)(2,1)} %bitcast.16), calls=%async_computation.1 | async-start | bytes 2097152 | tf_op jit(solution)/shard_map/all_to_all | solution.py:10
  43.7 0.0 copy-done
  43.8 0.1 broadcast_in_dim.60
  43.8 0.1 reshape.230
  43.9 0.0 copy-done.1
  43.9 0.1 broadcast_in_dim.61
  44.0 0.1 mul.51
  44.1 16.3 %all-to-all-done.1 = bf16[64,16,480]{2,1,0:T(8,128)(2,1)S(1)} async-done(((bf16[64,16,480]{2,1,0:T(8,128)(2,1)}), bf16[64,16,480]{2,1,0:T(8,128)(2,1)S(1)}, u32[]{:S(2)}, u32[]{:S(2)}) %all-to-all-start.1) | async-done | bytes 983072 | tf_op jit(solution)/shard_map/all_to_all | solution.py:10
  60.4 1.2 %multiply_convert_fusion = bf16[480,960]{1,0:T(8,128)(2,1)S(1)} fusion(bf16[1024,480]{1,0:T(8,128)(2,1)S(1)} %bitcast.46, s32[960]{0:T(1024)S(1)} %fusion.15, f32[960]{0:T(1024)S(1)} %mul.51), kind=kOutput, calls=%fused_computation.4 | convolution fusion | flops 945623040 | bytes 1912320 | tf_op jit(solution)/shard_map/dot_general | solution.py:51
  61.6 0.3 broadcast_in_dim.62
  61.9 0.0 copy-start.2
  61.9 0.0 copy-start.3
  61.9 8.3 %all_to_all.15 = bf16[2,480,960]{2,1,0:T(8,128)(2,1)S(1)} all-to-all(bf16[2,480,960]{2,1,0:T(8,128)(2,1)S(1)} %broadcast_in_dim.62), channel_id=1, replica_groups=mesh['pts'=64,'rows'=2] {'rows'}, dimensions={0} | all-to-all | bytes 3686400 | tf_op jit(solution)/shard_map/all_to_all | solution.py:10
  70.2 0.0 copy-done.2
  70.2 0.0 copy-done.3
  70.2 2.1 %fusion.2 = bf16[1,480,960]{2,1,0:T(8,128)(2,1)} fusion(bf16[960,960]{1,0:T(8,128)(2,1)S(1)} %bitcast.44, bf16[1,480,960]{2,1,0:T(8,128)(2,1)S(1)} %copy-done.2, f32[960]{0:T(1024)S(1)} %bitcast.54), kind=kOutput, calls=%fused_computation.8 | convolution fusion | flops 886579200 | bytes 3690240 | tf_op jit(solution)/shard_map/dot_general | solution.py:55
  (9 shorter events, 0.1 us)
Async XLA Ops:
  4.8 29.7 %all-to-all-start = ((bf16[64,16,480]{2,1,0:T(8,128)(2,1)}), bf16[64,16,480]{2,1,0:T(8,128)(2,1)S(1)}, u32[]{:S(2)}, u32[]{:S(2)}) async-start(bf16[64,16,480]{2,1,0:T(8,128)(2,1)} %copy.15), calls=%async_computation | async-start | bytes 2097152 | tf_op jit(solution)/shard_map/all_to_all | solution.py:10
  37.8 6.0 %copy-start = (s32[1,15]{1,0:T(1,128)S(1)}, s32[1,15]{1,0:T(1,128)}, u32[]{:S(2)}) copy-start(s32[1,15]{1,0:T(1,128)} %param.12) | copy-start | bytes 184
  37.8 6.1 %copy-start.1 = (f32[1,15]{1,0:T(1,128)S(1)}, f32[1,15]{1,0:T(1,128)}, u32[]{:S(2)}) copy-start(f32[1,15]{1,0:T(1,128)} %param.13) | copy-start | bytes 184
  39.1 21.3 %all-to-all-start.1 = ((bf16[64,16,480]{2,1,0:T(8,128)(2,1)}), bf16[64,16,480]{2,1,0:T(8,128)(2,1)S(1)}, u32[]{:S(2)}, u32[]{:S(2)}) async-start(bf16[64,16,480]{2,1,0:T(8,128)(2,1)} %bitcast.16), calls=%async_computation.1 | async-start | bytes 2097152 | tf_op jit(solution)/shard_map/all_to_all | solution.py:10
  61.9 8.3 %copy-start.2 = (bf16[1,480,960]{2,1,0:T(8,128)(2,1)S(1)}, bf16[1,480,960]{2,1,0:T(8,128)(2,1)}, u32[]{:S(2)}) copy-start(bf16[1,480,960]{2,1,0:T(8,128)(2,1)} %param.7) | copy-start | bytes 2764804
  61.9 8.3 %copy-start.3 = (f32[1,960]{1,0:T(1,128)S(1)}, f32[1,960]{1,0:T(1,128)}, u32[]{:S(2)}) copy-start(f32[1,960]{1,0:T(1,128)} %param.8) | copy-start | bytes 11524

commit v2 on v0

v2 whole, which is shorter than its diff:
```python
import functools

import jax
import jax.numpy as jnp
from jax import lax
from jax.experimental import pallas as pl
from jax.experimental.pallas import tpu as pltpu
from jax.sharding import PartitionSpec as P

MESH = pl.DeviceIdType.MESH
F32, BF16, I32 = jnp.float32, jnp.bfloat16, jnp.int32
FORMS, FREQS, POINTS, SIDE = 15, 64, 64, 4
LINES = 16
WIDTH = FORMS * FREQS
ROWS = WIDTH // 2
SLICES = ((0, 256), (256, 224))
PART = 256


def hops(delta):
    return sum(min(d, SIDE - d) for d in delta)


DELTAS = sorted(
    ((a, b, c) for a in range(SIDE) for b in range(SIDE) for c in range(SIDE) if (a, b, c) != (0, 0, 0)),
    key=lambda d: (-hops(d), (d[0] * 5 + d[1] * 11 + d[2] * 23) % 16),
)


def iota(shape, dim):
    return lax.broadcasted_iota(I32, shape, dim)


def remap_kernel(
    x_hbm, sb_ref, rs_ref, shift_ref, coef_ref, o_ref,
    x_ref, perm_ref, table_ref, ta, ra, ub, rb, pick_ref, shift_mat,
    load_sem, send_a, recv_a, send_b, recv_b, send_c, recv_c,
):
    me = lax.axis_index("pts")
    row = lax.axis_index("rows")
    mz, my, mx = me // (SIDE * SIDE), (me // SIDE) % SIDE, me % SIDE

    def peer(delta):
        dz, dy, dx = delta
        return (((mz + dz) % SIDE) * SIDE + (my + dy) % SIDE) * SIDE + (mx + dx) % SIDE

    barrier = pltpu.get_barrier_semaphore()
    for delta in DELTAS:
        pl.semaphore_signal(barrier, inc=1, device_id={"pts": peer(delta)}, device_id_type=MESH)
    pl.semaphore_signal(barrier, inc=1, device_id={"rows": 1 - row}, device_id_type=MESH)

    load = pltpu.make_async_copy(x_hbm, x_ref.at[pl.ds(0, ROWS)], load_sem)
    load.start()

    def build_perm(i, _):
        base = pl.multiple_of(i * 128, 128)
        line = iota((128, WIDTH), 0) + base
        want = jnp.where(line % LINES < FORMS, (line % LINES) * FREQS + line // LINES, -1)
        perm_ref[pl.ds(base, 128), :] = jnp.where(want == iota((128, WIDTH), 1), 1.0, 0.0).astype(BF16)
        return 0

    lax.fori_loop(0, FREQS * LINES // 128, build_perm, 0)
    table_ref[...] = jnp.zeros_like(table_ref)
    table_ref[0:1, 0:POINTS] = sb_ref[0:1, :].astype(F32)
    table_ref[0:1, POINTS : POINTS + FORMS] = rs_ref[...].astype(F32)
    table_ref[0:1, 128 : 128 + POINTS] = sb_ref[1:2, :].astype(F32)
    x_ref[ROWS:, :] = jnp.zeros((2 * PART - ROWS, WIDTH), BF16)
    load.wait()
    for s in range(2):
        block = lax.dot_general(
            perm_ref[...], x_ref[s * PART : (s + 1) * PART, :], (((1,), (1,)), ((), ())),
            preferred_element_type=F32,
        ).reshape(FREQS, LINES, PART)
        if s == 0:
            is_table = iota((FREQS, LINES, PART), 1) == FORMS
            block = jnp.where(is_table, table_ref[0:1, :].reshape(1, 1, PART), block)
        ta[s] = block.astype(BF16)
    pl.semaphore_wait(barrier, len(DELTAS) + 1)

    def copy_to(src, dst, send, recv, s, p):
        return pltpu.make_async_remote_copy(
            src_ref=src.at[s, p], dst_ref=dst.at[s, me], send_sem=send.at[s], recv_sem=recv.at[s],
            device_id={"pts": p}, device_id_type=MESH,
        )

    def send_all(src, dst, send, recv, s):
        for delta in DELTAS:
            copy_to(src, dst, send, recv, s, peer(delta)).start()
        dst[s, me] = src[s, me]

    def all_of(src, dst, send, recv, s):
        n = len(DELTAS)
        return pltpu.make_async_remote_copy(
            src_ref=src.at[s, pl.ds(0, n)], dst_ref=dst.at[s, pl.ds(0, n)], send_sem=send.at[s],
            recv_sem=recv.at[s], device_id={"pts": peer(DELTAS[0])}, device_id_type=MESH,
        )

    for s in range(2):
        send_all(ta, ra, send_a, recv_a, s)

    lane = iota((1, WIDTH), 1)
    moved_by = jnp.zeros((1, WIDTH), I32)
    weight = jnp.zeros((1, WIDTH), F32)
    for f in range(FORMS):
        here = lane // FREQS == f
        moved_by = jnp.where(here, shift_ref[0, f], moved_by)
        weight = jnp.where(here, coef_ref[0, f], weight)
    wanted_n = lane % FREQS + moved_by
    wanted = jnp.where((wanted_n >= 0) & (wanted_n < FREQS), wanted_n * LINES + lane // FREQS, -1)

    def build_shift(i, _):
        base = pl.multiple_of(i * 128, 128)
        line = iota((128, WIDTH), 0) + base
        shift_mat[pl.ds(base, 128), :] = jnp.where(line == wanted, 1.0, 0.0).astype(BF16)
        return 0

    lax.fori_loop(0, FREQS * LINES // 128, build_shift, 0)

    total = POINTS * LINES
    source = iota((POINTS, total), 1)
    widen = jnp.where(iota((POINTS, total), 0) == source // LINES, 1.0, 0.0).astype(BF16)
    form_of = (source % LINES).astype(F32)
    slot_of = (source // LINES * 2).astype(F32)

    for s in range(2):
        all_of(ta, ra, send_a, recv_a, s).wait_recv()
        if s == 0:
            tables = ra[0, :, FORMS, :].astype(F32)
            slots = []
            for c in range(2):
                held = lax.dot_general(
                    tables[:, c * 128 : c * 128 + 128].astype(BF16), widen, (((0,), (0,)), ((), ())),
                    preferred_element_type=F32,
                )[:POINTS]
                slots.append(jnp.where(held == form_of, slot_of + c, -7.0))
            table_ref[pl.ds(0, POINTS), 0:128] = tables[:, 0:128]
            for q in range(0, POINTS, 8):
                named = jnp.broadcast_to(
                    table_ref[q : q + 8, 0:128].reshape(8, 1, 128), (8, LINES, 128)
                ).reshape(8 * LINES, 128)
                f = iota((8 * LINES, 128), 0) % LINES
                at = iota((8 * LINES, 128), 1)
                named = jnp.sum(jnp.where(at == POINTS + f, named, 0.0), axis=1, keepdims=True)
                named = jnp.where(f[:, 0:1] == FORMS, -1.0, named)
                hit = None
                for c in range(2):
                    slot = jnp.broadcast_to(
                        slots[c][q : q + 8].reshape(8, 1, total), (8, LINES, total)
                    ).reshape(8 * LINES, total)
                    hit = (named == slot) if hit is None else hit | (named == slot)
                pick_ref[q * LINES : (q + 8) * LINES, :] = jnp.where(hit, 1.0, 0.0).astype(BF16)
        chosen = jnp.dot(
            pick_ref[...], ra[s].reshape(total, PART), preferred_element_type=F32
        )
        ub[s] = chosen.astype(BF16).reshape(POINTS, LINES, PART)
        send_all(ub, rb, send_b, recv_b, s)

    swaps = []
    for s, (first, size) in enumerate(SLICES):
        all_of(ub, rb, send_b, recv_b, s).wait_recv()
        moved = lax.dot_general(
            rb[s].reshape(FREQS * LINES, PART), shift_mat[...], (((0,), (0,)), ((), ())),
            preferred_element_type=F32,
        )
        where = o_ref.at[pl.ds(pl.multiple_of(row * ROWS + first, 32), size)]
        where[...] = (moved * weight).astype(BF16)[:size]
        swap = pltpu.make_async_remote_copy(
            src_ref=where, dst_ref=where, send_sem=send_c.at[s], recv_sem=recv_c.at[s],
            device_id={"rows": 1 - row}, device_id_type=MESH,
        )
        swap.start()
        swaps.append(swap)
    for s in range(2):
        all_of(ta, ra, send_a, recv_a, s).wait_send()
        all_of(ub, rb, send_b, recv_b, s).wait_send()
        swaps[s].wait()


def remap(x, sb, rs, shift, coef):
    vmem = pl.BlockSpec(memory_space=pltpu.VMEM)
    smem = pl.BlockSpec(memory_space=pltpu.SMEM)
    boxes = pltpu.VMEM((2, POINTS, LINES, PART), BF16)
    total = POINTS * LINES
    pair = pltpu.SemaphoreType.DMA((2,))
    return pl.pallas_call(
        remap_kernel,
        out_shape=jax.ShapeDtypeStruct((WIDTH, WIDTH), BF16),
        in_specs=[pl.BlockSpec(memory_space=pl.ANY), vmem, vmem, smem, smem],
        out_specs=vmem,
        scratch_shapes=[
            pltpu.VMEM((2 * PART, WIDTH), BF16),
            pltpu.VMEM((FREQS * LINES, WIDTH), BF16),
            pltpu.VMEM((POINTS, PART), F32),
            boxes, boxes, boxes, boxes,
            pltpu.VMEM((total, total), BF16),
            pltpu.VMEM((FREQS * LINES, WIDTH), BF16),
            pltpu.SemaphoreType.DMA, pair, pair, pair, pair, pair, pair,
        ],
        compiler_params=pltpu.CompilerParams(
            collective_id=0, has_side_effects=True, vmem_limit_bytes=48 * 1024 * 1024
        ),
        cost_estimate=pl.CostEstimate(flops=10**10, bytes_accessed=10**7, transcendentals=0),
    )(x, sb, rs, shift, coef)


def body(vertex, bubble, cross_deriv, send_blocks, recv_slots, freq_shift, proj_coef):
    remapped = remap(cross_deriv[0], send_blocks[0].T, recv_slots, freq_shift, proj_coef)
    scaled = (vertex[0].astype(F32) * bubble[0][None]).astype(BF16)
    out = jnp.dot(scaled, remapped, preferred_element_type=F32)
    return out.astype(BF16)[None]


def solution(mesh):
    in_specs = (
        P("pts", "rows", None),
        P("pts", None),
        P("pts", "rows", None),
        P("pts", None, None),
        P("pts", None),
        P("pts", None),
        P("pts", None),
    )
    out_specs = P("pts", "rows", None)
    return jax.shard_map(body, mesh=mesh, in_specs=in_specs, out_specs=out_specs, check_vma=False)
```

time: 162 us -> 44.1 us (0.27); the launches traced: 159 us -> 43.9 us
  waiting for transfers between devices: 116 us -> 0 us
  Pallas kernels: 0 us -> 37.9 us
  starting transfers between devices: 12.4 us -> 0 us
  local copies, waits for them, and re-layouts: 13.2 us -> 3.85 us
  other arithmetic: 8.69 us -> 0 us
  blocking collectives: 6.56 us -> 0 us
    all_to_all x1 -> x0, waiting for transfers between devices: 116 us -> none  [body(): lax.all_to_all(outgoing, 'pts', split_axis=0, concat_axis=0, tiled=True)]
    pallas_call x0 -> x1, Pallas kernels: none -> 37.9 us  [remap(): pl.pallas_call(remap_kernel, out_shape=jax.ShapeDtypeStruct((WIDTH, WIDTH...]
    all_to_all x1 -> x0, starting transfers between devices: 12.4 us -> none  [body(): lax.all_to_all(outgoing, 'pts', split_axis=0, concat_axis=0, tiled=True)]
    gather x2 -> x0, local copies, waits for them, and re-layouts: 10.2 us -> none  [the longest x1 6.23 us: body(): local_boxes[jnp.clip(wanted, 0, points * form_count - 1)]]
    select_n x2 -> x0, other arithmetic: 7.92 us -> none  [the longest x1 7.24 us: body(): jnp.where((wanted >= 0)[:, :, None, None], local_boxes[jnp.clip(wanted, 0...]
    all_to_all x1 -> x0, blocking collectives: 6.56 us -> none  [copy_for_each(): return lax.all_to_all(copies, axis, split_axis=0, concat_axis=0, tiled=True)]
    unnamed x11 -> x14, local copies, waits for them, and re-layouts: 1.7 us -> 3.85 us
  transfers between devices with their start and end apart: 1 -> 0, of which waited for: 1 -> 0; matrix products, arithmetic and copies ran while one was open for 0% -> 0% of each run, Pallas kernels for 0% -> 0%
where the time goes in v2:
time: 44.1 us; the launch traced here: 43.9 us
  Pallas kernels  37.9 us (86%)
  local copies, waits for them, and re-layouts  3.85 us (9%)
  matrix products  2.13 us (5%)
    pallas_call x1, Pallas kernels, remap(): pl.pallas_call(remap_kernel, out_shape=jax.ShapeDtypeStruct((WIDTH, WIDTH...  37.9 us
    unnamed x14, local copies, waits for them, and re-layouts  3.85 us
    dot_general x1, matrix products, body(): out = jnp.dot(scaled, remapped, preferred_element_type=F32)  2.13 us

profile of v2, /device:TPU:1, one launch (start us, length us, event | category | flops | bytes accessed | tf_op | source)
XLA Modules:
  0.0 43.9 jit_solution(6526017806045556682)
XLA Ops:
  0.0 0.0 copy-start
  0.0 1.2 %copy-done = bf16[1,480,960]{2,1,0:T(8,128)(2,1)S(1)} copy-done((bf16[1,480,960]{2,1,0:T(8,128)(2,1)S(1)}, bf16[1,480,960]{2,1,0:T(8,128)(2,1)}, u32[]{:S(2)}) %copy-start) | copy-done | bytes 921624
  1.2 0.0 copy-start.1
  1.2 0.7 %copy-done.1 = s32[1,64,2]{1,2,0:T(2,128)S(1)} copy-done((s32[1,64,2]{1,2,0:T(2,128)S(1)}, s32[1,64,2]{1,2,0:T(2,128)}, u32[]{:S(2)}) %copy-start.1) | copy-done | bytes 536
  1.9 0.0 copy-start.2
  1.9 0.7 %copy-done.2 = s32[1,15]{1,0:T(1,128)S(1)} copy-done((s32[1,15]{1,0:T(1,128)S(1)}, s32[1,15]{1,0:T(1,128)}, u32[]{:S(2)}) %copy-start.2) | copy-done | bytes 84
  2.5 0.0 copy-start.3
  2.5 0.7 %copy-done.3 = s32[1,15]{1,0:T(1,128)S(1)} copy-done((s32[1,15]{1,0:T(1,128)S(1)}, s32[1,15]{1,0:T(1,128)}, u32[]{:S(2)}) %copy-start.3) | copy-done | bytes 84
  3.2 0.0 copy-start.4
  3.2 0.7 %copy-done.4 = f32[1,15]{1,0:T(1,128)S(1)} copy-done((f32[1,15]{1,0:T(1,128)S(1)}, f32[1,15]{1,0:T(1,128)}, u32[]{:S(2)}) %copy-start.4) | copy-done | bytes 84
  3.8 0.0 copy-start.5
  3.9 0.0 copy-start.6
  3.9 37.9 %shard_map.73 = bf16[960,960]{1,0:T(8,128)(2,1)S(1)} custom-call(bf16[480,960]{1,0:T(8,128)(2,1)S(1)} %bitcast.14, s32[2,64]{1,0:T(2,128)S(1)} %bitcast.15, s32[1,15]{1,0:T(1,128)S(1)} %copy-done.2, s32[1,15]{1,0:T(1,128)S(1)} %copy-done.3, f32[1,15]{1,0:T(1,128)S(1)} %copy-done.4), custom_call_target="tpu_custom_call" | custom-call | flops 10000000000 | bytes 10000000 | tf_op jit(solution)/shard_map/pallas_call | solution.py:185
  41.7 0.0 copy-done.5
  41.7 0.0 copy-done.6
  41.8 2.1 %fusion.1 = bf16[1,480,960]{2,1,0:T(8,128)(2,1)} fusion(bf16[960,960]{1,0:T(8,128)(2,1)S(1)} %shard_map.73, bf16[1,480,960]{2,1,0:T(8,128)(2,1)S(1)} %copy-done.5, f32[960]{0:T(1024)S(1)} %bitcast.16), kind=kOutput, calls=%fused_computation.3 | convolution fusion | flops 886579200 | bytes 3690240 | tf_op jit(solution)/shard_map/dot_general | solution.py:209
Async XLA Ops:
  0.0 1.2 %copy-start = (bf16[1,480,960]{2,1,0:T(8,128)(2,1)S(1)}, bf16[1,480,960]{2,1,0:T(8,128)(2,1)}, u32[]{:S(2)}) copy-start(bf16[1,480,960]{2,1,0:T(8,128)(2,1)} %param.9) | copy-start | bytes 2764804
  1.2 0.7 %copy-start.1 = (s32[1,64,2]{1,2,0:T(2,128)S(1)}, s32[1,64,2]{1,2,0:T(2,128)}, u32[]{:S(2)}) copy-start(s32[1,64,2]{1,2,0:T(2,128)} %param.10) | copy-start | bytes 1540
  1.9 0.7 %copy-start.2 = (s32[1,15]{1,0:T(1,128)S(1)}, s32[1,15]{1,0:T(1,128)}, u32[]{:S(2)}) copy-start(s32[1,15]{1,0:T(1,128)} %rs_ref.1) | copy-start | bytes 184
  2.5 0.7 %copy-start.3 = (s32[1,15]{1,0:T(1,128)S(1)}, s32[1,15]{1,0:T(1,128)}, u32[]{:S(2)}) copy-start(s32[1,15]{1,0:T(1,128)} %shift_ref.1) | copy-start | bytes 184
  3.2 0.7 %copy-start.4 = (f32[1,15]{1,0:T(1,128)S(1)}, f32[1,15]{1,0:T(1,128)}, u32[]{:S(2)}) copy-start(f32[1,15]{1,0:T(1,128)} %coef_ref.1) | copy-start | bytes 184
  3.8 37.9 %copy-start.5 = (bf16[1,480,960]{2,1,0:T(8,128)(2,1)S(1)}, bf16[1,480,960]{2,1,0:T(8,128)(2,1)}, u32[]{:S(2)}) copy-start(bf16[1,480,960]{2,1,0:T(8,128)(2,1)} %param.7) | copy-start | bytes 2764804
  3.9 37.9 %copy-start.6 = (f32[1,960]{1,0:T(1,128)S(1)}, f32[1,960]{1,0:T(1,128)}, u32[]{:S(2)}) copy-start(f32[1,960]{1,0:T(1,128)} %param.8) | copy-start | bytes 11524

commit v3 on v2

--- a/solution.py
+++ b/solution.py
@@ -13,7 +13,6 @@
 LINES = 16
 WIDTH = FORMS * FREQS
 ROWS = WIDTH // 2
-SLICES = ((0, 256), (256, 224))
 PART = 256
 
 
@@ -32,8 +31,9 @@
 
 
 def remap_kernel(
-    x_hbm, sb_ref, rs_ref, shift_ref, coef_ref, o_ref,
-    x_ref, perm_ref, table_ref, ta, ra, ub, rb, pick_ref, shift_mat,
+    x_hbm, v_hbm, bub_hbm, sb_hbm, rs_hbm, shift_hbm, coef_hbm, o_ref,
+    x_ref, v_ref, bub_ref, sb_ref, rs_ref, shift_ref, coef_ref, perm_ref, table_ref, ta, ra, ub, rb,
+    pick_ref, shift_mat, wide_ref, halves, remapped, acc_ref,
     load_sem, send_a, recv_a, send_b, recv_b, send_c, recv_c,
 ):
     me = lax.axis_index("pts")
@@ -49,24 +49,35 @@
         pl.semaphore_signal(barrier, inc=1, device_id={"pts": peer(delta)}, device_id_type=MESH)
     pl.semaphore_signal(barrier, inc=1, device_id={"rows": 1 - row}, device_id_type=MESH)
 
-    load = pltpu.make_async_copy(x_hbm, x_ref.at[pl.ds(0, ROWS)], load_sem)
-    load.start()
+    loads = [
+        pltpu.make_async_copy(src, dst, load_sem.at[i])
+        for i, (src, dst) in enumerate((
+            (x_hbm, x_ref.at[pl.ds(0, ROWS)]), (sb_hbm, sb_ref), (rs_hbm, rs_ref), (shift_hbm, shift_ref),
+            (coef_hbm, coef_ref), (bub_hbm, bub_ref), (v_hbm, v_ref),
+        ))
+    ]
+    for load in loads:
+        load.start()
 
     def build_perm(i, _):
         base = pl.multiple_of(i * 128, 128)
-        line = iota((128, WIDTH), 0) + base
-        want = jnp.where(line % LINES < FORMS, (line % LINES) * FREQS + line // LINES, -1)
+        line = iota((128, 1), 0) + base
+        g = line & (LINES - 1)
+        want = jnp.where(g < FORMS, g * FREQS + (line >> 4), -1)
         perm_ref[pl.ds(base, 128), :] = jnp.where(want == iota((128, WIDTH), 1), 1.0, 0.0).astype(BF16)
         return 0
 
     lax.fori_loop(0, FREQS * LINES // 128, build_perm, 0)
     table_ref[...] = jnp.zeros_like(table_ref)
+    loads[1].wait()
+    loads[2].wait()
     table_ref[0:1, 0:POINTS] = sb_ref[0:1, :].astype(F32)
     table_ref[0:1, POINTS : POINTS + FORMS] = rs_ref[...].astype(F32)
     table_ref[0:1, 128 : 128 + POINTS] = sb_ref[1:2, :].astype(F32)
     x_ref[ROWS:, :] = jnp.zeros((2 * PART - ROWS, WIDTH), BF16)
-    load.wait()
-    for s in range(2):
+    loads[0].wait()
+
+    def permute(s):
         block = lax.dot_general(
             perm_ref[...], x_ref[s * PART : (s + 1) * PART, :], (((1,), (1,)), ((), ())),
             preferred_element_type=F32,
@@ -75,6 +86,8 @@
             is_table = iota((FREQS, LINES, PART), 1) == FORMS
             block = jnp.where(is_table, table_ref[0:1, :].reshape(1, 1, PART), block)
         ta[s] = block.astype(BF16)
+
+    permute(0)
     pl.semaphore_wait(barrier, len(DELTAS) + 1)
 
     def copy_to(src, dst, send, recv, s, p):
@@ -95,18 +108,33 @@
             recv_sem=recv.at[s], device_id={"pts": peer(DELTAS[0])}, device_id_type=MESH,
         )
 
-    for s in range(2):
-        send_all(ta, ra, send_a, recv_a, s)
-
+    send_all(ta, ra, send_a, recv_a, 0)
+    permute(1)
+    send_all(ta, ra, send_a, recv_a, 1)
+
+    for load in loads[3:]:
+        load.wait()
+    wide_ref[:, 896:] = jnp.zeros((32, 128), F32)
+
+    def build_halves(i, _):
+        at = pl.ds(pl.multiple_of(i * 32, 32), 32)
+        scaled = (v_ref[at, :].astype(F32) * bub_ref[...]).astype(BF16).astype(F32)
+        wide_ref[:, :WIDTH] = scaled
+        inside = iota((32, 2 * PART), 1) < ROWS
+        halves[0, at, :] = jnp.where(inside, wide_ref[:, : 2 * PART], 0.0).astype(BF16)
+        halves[1, at, :] = pltpu.roll(wide_ref[...], 1024 - ROWS, 1)[:, : 2 * PART].astype(BF16)
+        return 0
+
+    lax.fori_loop(0, ROWS // 32, build_halves, 0)
     lane = iota((1, WIDTH), 1)
     moved_by = jnp.zeros((1, WIDTH), I32)
     weight = jnp.zeros((1, WIDTH), F32)
     for f in range(FORMS):
-        here = lane // FREQS == f
+        here = (lane >> 6) == f
         moved_by = jnp.where(here, shift_ref[0, f], moved_by)
         weight = jnp.where(here, coef_ref[0, f], weight)
-    wanted_n = lane % FREQS + moved_by
-    wanted = jnp.where((wanted_n >= 0) & (wanted_n < FREQS), wanted_n * LINES + lane // FREQS, -1)
+    wanted_n = (lane & (FREQS - 1)) + moved_by
+    wanted = jnp.where((wanted_n >= 0) & (wanted_n < FREQS), wanted_n * LINES + (lane >> 6), -1)
 
     def build_shift(i, _):
         base = pl.multiple_of(i * 128, 128)
@@ -118,9 +146,9 @@
 
     total = POINTS * LINES
     source = iota((POINTS, total), 1)
-    widen = jnp.where(iota((POINTS, total), 0) == source // LINES, 1.0, 0.0).astype(BF16)
-    form_of = (source % LINES).astype(F32)
-    slot_of = (source // LINES * 2).astype(F32)
+    widen = jnp.where(iota((POINTS, total), 0) == (source >> 4), 1.0, 0.0).astype(BF16)
+    form_of = (source & (LINES - 1)).astype(F32)
+    slot_of = ((source >> 4) * 2).astype(F32)
 
     for s in range(2):
         all_of(ta, ra, send_a, recv_a, s).wait_recv()
@@ -138,7 +166,7 @@
                 named = jnp.broadcast_to(
                     table_ref[q : q + 8, 0:128].reshape(8, 1, 128), (8, LINES, 128)
                 ).reshape(8 * LINES, 128)
-                f = iota((8 * LINES, 128), 0) % LINES
+                f = iota((8 * LINES, 128), 0) & (LINES - 1)
                 at = iota((8 * LINES, 128), 1)
                 named = jnp.sum(jnp.where(at == POINTS + f, named, 0.0), axis=1, keepdims=True)
                 named = jnp.where(f[:, 0:1] == FORMS, -1.0, named)
@@ -156,58 +184,81 @@
         send_all(ub, rb, send_b, recv_b, s)
 
     swaps = []
-    for s, (first, size) in enumerate(SLICES):
+    for s in range(2):
         all_of(ub, rb, send_b, recv_b, s).wait_recv()
         moved = lax.dot_general(
             rb[s].reshape(FREQS * LINES, PART), shift_mat[...], (((0,), (0,)), ((), ())),
             preferred_element_type=F32,
         )
-        where = o_ref.at[pl.ds(pl.multiple_of(row * ROWS + first, 32), size)]
-        where[...] = (moved * weight).astype(BF16)[:size]
+        remapped[row, s] = (moved * weight).astype(BF16)
         swap = pltpu.make_async_remote_copy(
-            src_ref=where, dst_ref=where, send_sem=send_c.at[s], recv_sem=recv_c.at[s],
-            device_id={"rows": 1 - row}, device_id_type=MESH,
+            src_ref=remapped.at[row, s], dst_ref=remapped.at[row, s], send_sem=send_c.at[s],
+            recv_sem=recv_c.at[s], device_id={"rows": 1 - row}, device_id_type=MESH,
         )
         swap.start()
         swaps.append(swap)
+
+        def times(half):
+            return jnp.dot(
+                halves[half, :, s * PART : (s + 1) * PART], remapped[half, s], preferred_element_type=F32
+            )
+
+        if s == 0:
+            acc_ref[...] = times(row)
+        else:
+            acc_ref[...] += times(row)
+        swap.wait_recv()
+        if s == 0:
+            acc_ref[...] += times(1 - row)
+        else:
+            o_ref[...] = (acc_ref[...] + times(1 - row)).astype(BF16)
     for s in range(2):
         all_of(ta, ra, send_a, recv_a, s).wait_send()
         all_of(ub, rb, send_b, recv_b, s).wait_send()
-        swaps[s].wait()
-
-
-def remap(x, sb, rs, shift, coef):
+        swaps[s].wait_send()
+
+
+def remap(x, vertex, bubble, sb, rs, shift, coef):
     vmem = pl.BlockSpec(memory_space=pltpu.VMEM)
-    smem = pl.BlockSpec(memory_space=pltpu.SMEM)
     boxes = pltpu.VMEM((2, POINTS, LINES, PART), BF16)
     total = POINTS * LINES
     pair = pltpu.SemaphoreType.DMA((2,))
     return pl.pallas_call(
         remap_kernel,
-        out_shape=jax.ShapeDtypeStruct((WIDTH, WIDTH), BF16),
-        in_specs=[pl.BlockSpec(memory_space=pl.ANY), vmem, vmem, smem, smem],
+        out_shape=jax.ShapeDtypeStruct((ROWS, WIDTH), BF16),
+        in_specs=[pl.BlockSpec(memory_space=pl.ANY)] * 7,
         out_specs=vmem,
         scratch_shapes=[
             pltpu.VMEM((2 * PART, WIDTH), BF16),
+            pltpu.VMEM((ROWS, WIDTH), BF16),
+            pltpu.VMEM((1, WIDTH), F32),
+            pltpu.VMEM((2, POINTS), I32),
+            pltpu.VMEM((1, FORMS), I32),
+            pltpu.SMEM((1, FORMS), I32),
+            pltpu.SMEM((1, FORMS), F32),
             pltpu.VMEM((FREQS * LINES, WIDTH), BF16),
             pltpu.VMEM((POINTS, PART), F32),
             boxes, boxes, boxes, boxes,
             pltpu.VMEM((total, total), BF16),
             pltpu.VMEM((FREQS * LINES, WIDTH), BF16),
-            pltpu.SemaphoreType.DMA, pair, pair, pair, pair, pair, pair,
+            pltpu.VMEM((32, 1024), F32),
+            pltpu.VMEM((2, ROWS, 2 * PART), BF16),
+            pltpu.VMEM((2, 2, PART, WIDTH), BF16),
+            pltpu.VMEM((ROWS, WIDTH), F32),
+            pltpu.SemaphoreType.DMA((7,)), pair, pair, pair, pair, pair, pair,
         ],
         compiler_params=pltpu.CompilerParams(
-            collective_id=0, has_side_effects=True, vmem_limit_bytes=48 * 1024 * 1024
+            collective_id=0, has_side_effects=True, vmem_limit_bytes=62 * 1024 * 1024
         ),
         cost_estimate=pl.CostEstimate(flops=10**10, bytes_accessed=10**7, transcendentals=0),
-    )(x, sb, rs, shift, coef)
+    )(x, vertex, bubble, sb, rs, shift, coef)
 
 
 def body(vertex, bubble, cross_deriv, send_blocks, recv_slots, freq_shift, proj_coef):
-    remapped = remap(cross_deriv[0], send_blocks[0].T, recv_slots, freq_shift, proj_coef)
-    scaled = (vertex[0].astype(F32) * bubble[0][None]).astype(BF16)
-    out = jnp.dot(scaled, remapped, preferred_element_type=F32)
-    return out.astype(BF16)[None]
+    out = remap(
+        cross_deriv[0], vertex[0], bubble, send_blocks[0].T, recv_slots, freq_shift, proj_coef
+    )
+    return out[None]
 
 
 def solution(mesh):

time: 44.1 us -> 41.5 us (0.941)
  matrix products: 2.13 us -> 0 us
  local copies, waits for them, and re-layouts: 3.85 us -> 2.21 us
  Pallas kernels: 37.9 us -> 38.9 us
    dot_general x1 -> x0, matrix products: 2.13 us -> none  [body(): out = jnp.dot(scaled, remapped, preferred_element_type=F32)]
    unnamed x14 -> x1, local copies, waits for them, and re-layouts: 3.85 us -> 2.21 us
    pallas_call x1, Pallas kernels: 37.9 us -> 38.9 us  [remap(): pl.pallas_call(remap_kernel, out_shape=jax.ShapeDtypeStruct((ROWS, WIDTH)...]
where the time goes in v3:
time: 41.5 us; the launch traced here: 41.2 us
  Pallas kernels  38.9 us (94%)
  local copies, waits for them, and re-layouts  2.21 us (5%)
    pallas_call x1, Pallas kernels, remap(): pl.pallas_call(remap_kernel, out_shape=jax.ShapeDtypeStruct((ROWS, WIDTH)...  38.9 us
    unnamed x1, local copies, waits for them, and re-layouts  2.21 us

profile of v3, /device:TPU:1, one launch (start us, length us, event | category | flops | bytes accessed | tf_op | source)
XLA Modules:
  0.0 41.2 jit_solution(1450414148119886768)
XLA Ops:
  0.0 38.9 %shard_map.73 = bf16[480,960]{1,0:T(8,128)(2,1)} custom-call(bf16[480,960]{1,0:T(8,128)(2,1)} %bitcast.7, bf16[480,960]{1,0:T(8,128)(2,1)} %bitcast.8, f32[1,960]{1,0:T(1,128)} %bub_hbm.1, s32[2,64]{1,0:T(2,128)} %bitcast.9, s32[1,15]{1,0:T(1,128)} %rs_hbm.1, s32[1,15]{1,0:T(1,128)} %shift_hbm.1, f32[1,15]{1,0:T(1,128)} %coef_hbm.1), custom_call_target="tpu_custom_call" | custom-call | flops 10000000000 | bytes 10000000 | tf_op jit(solution)/shard_map/pallas_call | solution.py:226
  39.0 2.2 %copy.9 = bf16[1,480,960]{2,1,0:T(8,128)(2,1)} copy(bf16[1,480,960]{2,1,0:T(8,128)(2,1)} %bitcast.6) | data formatting | bytes 1843200

commit v4 on v3

--- a/solution.py
+++ b/solution.py
@@ -13,6 +13,7 @@
 LINES = 16
 WIDTH = FORMS * FREQS
 ROWS = WIDTH // 2
+OUT_BLOCKS = 3
 PART = 256
 
 
@@ -22,7 +23,7 @@
 
 DELTAS = sorted(
     ((a, b, c) for a in range(SIDE) for b in range(SIDE) for c in range(SIDE) if (a, b, c) != (0, 0, 0)),
-    key=lambda d: (-hops(d), (d[0] * 5 + d[1] * 11 + d[2] * 23) % 16),
+    key=lambda d: (-hops(d), d),
 )
 
 
@@ -33,8 +34,8 @@
 def remap_kernel(
     x_hbm, v_hbm, bub_hbm, sb_hbm, rs_hbm, shift_hbm, coef_hbm, o_ref,
     x_ref, v_ref, bub_ref, sb_ref, rs_ref, shift_ref, coef_ref, perm_ref, table_ref, ta, ra, ub, rb,
-    pick_ref, shift_mat, wide_ref, halves, remapped, acc_ref,
-    load_sem, send_a, recv_a, send_b, recv_b, send_c, recv_c,
+    pick_ref, shift_mat, wide_ref, halves, remapped, acc_ref, out_ref,
+    load_sem, send_a, recv_a, send_b, recv_b, send_c, recv_c, store_sem,
 ):
     me = lax.axis_index("pts")
     row = lax.axis_index("rows")
@@ -43,11 +44,6 @@
     def peer(delta):
         dz, dy, dx = delta
         return (((mz + dz) % SIDE) * SIDE + (my + dy) % SIDE) * SIDE + (mx + dx) % SIDE
-
-    barrier = pltpu.get_barrier_semaphore()
-    for delta in DELTAS:
-        pl.semaphore_signal(barrier, inc=1, device_id={"pts": peer(delta)}, device_id_type=MESH)
-    pl.semaphore_signal(barrier, inc=1, device_id={"rows": 1 - row}, device_id_type=MESH)
 
     loads = [
         pltpu.make_async_copy(src, dst, load_sem.at[i])
@@ -58,6 +54,11 @@
     ]
     for load in loads:
         load.start()
+
+    barrier = pltpu.get_barrier_semaphore()
+    for delta in DELTAS:
+        pl.semaphore_signal(barrier, inc=1, device_id={"pts": peer(delta)}, device_id_type=MESH)
+    pl.semaphore_signal(barrier, inc=1, device_id={"rows": 1 - row}, device_id_type=MESH)
 
     def build_perm(i, _):
         base = pl.multiple_of(i * 128, 128)
@@ -177,13 +178,21 @@
                     ).reshape(8 * LINES, total)
                     hit = (named == slot) if hit is None else hit | (named == slot)
                 pick_ref[q * LINES : (q + 8) * LINES, :] = jnp.where(hit, 1.0, 0.0).astype(BF16)
-        chosen = jnp.dot(
-            pick_ref[...], ra[s].reshape(total, PART), preferred_element_type=F32
-        )
-        ub[s] = chosen.astype(BF16).reshape(POINTS, LINES, PART)
+        for h in range(2):
+            chosen = jnp.dot(
+                pick_ref[h * total // 2 : (h + 1) * total // 2, :], ra[s].reshape(total, PART),
+                preferred_element_type=F32,
+            )
+            chosen = chosen.astype(BF16).reshape(POINTS // 2, LINES, PART)
+            ub[s, h * POINTS // 2 : (h + 1) * POINTS // 2] = chosen
         send_all(ub, rb, send_b, recv_b, s)
 
-    swaps = []
+    def times(half, s, rows=slice(None)):
+        return jnp.dot(
+            halves[half, rows, s * PART : (s + 1) * PART], remapped[half, s], preferred_element_type=F32
+        )
+
+    swaps, stores = [], []
     for s in range(2):
         all_of(ub, rb, send_b, recv_b, s).wait_recv()
         moved = lax.dot_general(
@@ -197,29 +206,29 @@
         )
         swap.start()
         swaps.append(swap)
-
-        def times(half):
-            return jnp.dot(
-                halves[half, :, s * PART : (s + 1) * PART], remapped[half, s], preferred_element_type=F32
-            )
-
         if s == 0:
-            acc_ref[...] = times(row)
+            acc_ref[...] = times(row, s)
         else:
-            acc_ref[...] += times(row)
-        swap.wait_recv()
-        if s == 0:
-            acc_ref[...] += times(1 - row)
-        else:
-            o_ref[...] = (acc_ref[...] + times(1 - row)).astype(BF16)
+            acc_ref[...] += times(row, s)
+    swaps[0].wait_recv()
+    acc_ref[...] += times(1 - row, 0)
+    swaps[1].wait_recv()
+    step = ROWS // OUT_BLOCKS
+    for b in range(OUT_BLOCKS):
+        rows = slice(b * step, (b + 1) * step)
+        out_ref[rows, :] = (acc_ref[rows, :] + times(1 - row, 1, rows)).astype(BF16)
+        at = pl.ds(b * step, step)
+        stores.append(pltpu.make_async_copy(out_ref.at[at], o_ref.at[at], store_sem.at[b]))
+        stores[-1].start()
     for s in range(2):
         all_of(ta, ra, send_a, recv_a, s).wait_send()
         all_of(ub, rb, send_b, recv_b, s).wait_send()
         swaps[s].wait_send()
+    for store in stores:
+        store.wait()
 
 
 def remap(x, vertex, bubble, sb, rs, shift, coef):
-    vmem = pl.BlockSpec(memory_space=pltpu.VMEM)
     boxes = pltpu.VMEM((2, POINTS, LINES, PART), BF16)
     total = POINTS * LINES
     pair = pltpu.SemaphoreType.DMA((2,))
@@ -227,7 +236,7 @@
         remap_kernel,
         out_shape=jax.ShapeDtypeStruct((ROWS, WIDTH), BF16),
         in_specs=[pl.BlockSpec(memory_space=pl.ANY)] * 7,
-        out_specs=vmem,
+        out_specs=pl.BlockSpec(memory_space=pl.ANY),
         scratch_shapes=[
             pltpu.VMEM((2 * PART, WIDTH), BF16),
             pltpu.VMEM((ROWS, WIDTH), BF16),
@@ -245,7 +254,9 @@
             pltpu.VMEM((2, ROWS, 2 * PART), BF16),
             pltpu.VMEM((2, 2, PART, WIDTH), BF16),
             pltpu.VMEM((ROWS, WIDTH), F32),
+            pltpu.VMEM((ROWS, WIDTH), BF16),
             pltpu.SemaphoreType.DMA((7,)), pair, pair, pair, pair, pair, pair,
+            pltpu.SemaphoreType.DMA((OUT_BLOCKS,)),
         ],
         compiler_params=pltpu.CompilerParams(
             collective_id=0, has_side_effects=True, vmem_limit_bytes=62 * 1024 * 1024

time: 41.5 us -> 41 us (0.988)
  no operation moved by 1% of the time
where the time goes in v4:
time: 41 us; the launch traced here: 40.9 us
  Pallas kernels  38.7 us (94%)
  local copies, waits for them, and re-layouts  2.21 us (5%)
    pallas_call x1, Pallas kernels, remap(): pl.pallas_call(remap_kernel, out_shape=jax.ShapeDtypeStruct((ROWS, WIDTH)...  38.7 us
    unnamed x1, local copies, waits for them, and re-layouts  2.21 us

profile of v4, /device:TPU:1, one launch (start us, length us, event | category | flops | bytes accessed | tf_op | source)
XLA Modules:
  0.0 40.9 jit_solution(3090877428176335824)
XLA Ops:
  0.0 38.7 %shard_map.73 = bf16[480,960]{1,0:T(8,128)(2,1)} custom-call(bf16[480,960]{1,0:T(8,128)(2,1)} %bitcast.7, bf16[480,960]{1,0:T(8,128)(2,1)} %bitcast.8, f32[1,960]{1,0:T(1,128)} %bub_hbm.1, s32[2,64]{1,0:T(2,128)} %bitcast.9, s32[1,15]{1,0:T(1,128)} %rs_hbm.1, s32[1,15]{1,0:T(1,128)} %shift_hbm.1, f32[1,15]{1,0:T(1,128)} %coef_hbm.1), custom_call_target="tpu_custom_call" | custom-call | flops 10000000000 | bytes 10000000 | tf_op jit(solution)/shard_map/pallas_call | solution.py:235
  38.7 2.2 %copy.9 = bf16[1,480,960]{2,1,0:T(8,128)(2,1)} copy(bf16[1,480,960]{2,1,0:T(8,128)(2,1)} %bitcast.6) | data formatting | bytes 1843200

commit v5 on v4

--- a/solution.py
+++ b/solution.py
@@ -14,6 +14,7 @@
 WIDTH = FORMS * FREQS
 ROWS = WIDTH // 2
 OUT_BLOCKS = 3
+USED = (256, 224)
 PART = 256
 
 
@@ -189,7 +190,8 @@
 
     def times(half, s, rows=slice(None)):
         return jnp.dot(
-            halves[half, rows, s * PART : (s + 1) * PART], remapped[half, s], preferred_element_type=F32
+            halves[half, rows, s * PART : s * PART + USED[s]], remapped[half, s, : USED[s]],
+            preferred_element_type=F32,
         )
 
     swaps, stores = [], []
@@ -199,9 +201,10 @@
             rb[s].reshape(FREQS * LINES, PART), shift_mat[...], (((0,), (0,)), ((), ())),
             preferred_element_type=F32,
         )
-        remapped[row, s] = (moved * weight).astype(BF16)
+        remapped[row, s, : USED[s]] = (moved * weight).astype(BF16)[: USED[s]]
+        where = remapped.at[row, s, pl.ds(0, USED[s])]
         swap = pltpu.make_async_remote_copy(
-            src_ref=remapped.at[row, s], dst_ref=remapped.at[row, s], send_sem=send_c.at[s],
+            src_ref=where, dst_ref=where, send_sem=send_c.at[s],
             recv_sem=recv_c.at[s], device_id={"rows": 1 - row}, device_id_type=MESH,
         )
         swap.start()

time: 41 us -> 40.9 us (level)
  no operation moved by 1% of the time
where the time goes in v5:
time: 40.9 us; the launch traced here: 40.8 us
  Pallas kernels  38.5 us (94%)
  local copies, waits for them, and re-layouts  2.21 us (5%)
    pallas_call x1, Pallas kernels, remap(): pl.pallas_call(remap_kernel, out_shape=jax.ShapeDtypeStruct((ROWS, WIDTH)...  38.5 us
    unnamed x1, local copies, waits for them, and re-layouts  2.21 us

profile of v5, /device:TPU:1, one launch (start us, length us, event | category | flops | bytes accessed | tf_op | source)
XLA Modules:
  0.0 40.8 jit_solution(18135336917320050944)
XLA Ops:
  0.0 38.5 %shard_map.73 = bf16[480,960]{1,0:T(8,128)(2,1)} custom-call(bf16[480,960]{1,0:T(8,128)(2,1)} %bitcast.7, bf16[480,960]{1,0:T(8,128)(2,1)} %bitcast.8, f32[1,960]{1,0:T(1,128)} %bub_hbm.1, s32[2,64]{1,0:T(2,128)} %bitcast.9, s32[1,15]{1,0:T(1,128)} %rs_hbm.1, s32[1,15]{1,0:T(1,128)} %shift_hbm.1, f32[1,15]{1,0:T(1,128)} %coef_hbm.1), custom_call_target="tpu_custom_call" | custom-call | flops 10000000000 | bytes 10000000 | tf_op jit(solution)/shard_map/pallas_call | solution.py:238
  38.6 2.2 %copy.9 = bf16[1,480,960]{2,1,0:T(8,128)(2,1)} copy(bf16[1,480,960]{2,1,0:T(8,128)(2,1)} %bitcast.6) | data formatting | bytes 1843200
